TPU v7x, 512 devices: a 4x2x32 block of a 4x8x32 slice. The times are simulated.
512 devices in a mesh: group: 2 (over y), ctx: 64 (over z, core), head: 4 (over x).
Axes of the slice: x: 4, y: 2, z: 32, core: 2. Of those that a mesh axis runs over, the one named last changes fastest.
The devices are a block of a 4x8x32 slice.
Arguments:
- query_nope: bfloat16 [8192, 8192], P(('group', 'ctx'), 'head'), parts along dimension 0, may hold values from -6 to 6
- query_rope: bfloat16 [8192, 4096], P(('group', 'ctx'), 'head'), parts along dimension 0, may hold values from -16 to 16
- kv_latent: bfloat16 [8192, 512], P(('group', 'ctx'), 'head'), parts along dimension 0, may hold values from -1300 to 1300
- key_rope: bfloat16 [8192, 64], P(('group', 'ctx')), parts along dimension 0, may hold values from -16 to 16
- latent_gain: float32 [512], replicated, may hold values from 0.1 to 1.9
- w_key: bfloat16 [512, 8192], P(None, 'head'), may hold values from -0.25 to 0.25
- w_value: bfloat16 [512, 8192], P(None, 'head'), may hold values from -0.25 to 0.25
- block_order: int32 [256], P('group'), parts along dimension 0, may hold values from 0 to 127, as said below
Outputs:
- attention_out: bfloat16 [8192, 8192], P(('group', 'ctx'), 'head'), parts along dimension 0
There are 2 independent parts, one for each index of `group`. A program takes and returns all parts, laid end to end along the dimension named above; an argument that names none is the same for every part. Nothing has to cross between parts.
Inputs may be any that keep to these rules, and one draw needn't show every extreme that they name: `block_order`: A permutation of 0 to 127. Entries 2 c and 2 c + 1, for each c < 64, add up to 127.
All inputs are finite; a program needn't handle non-finite values.
Results may differ from a plain program's by a relative error of at most 0.0081.
Values may be sent and summed in bfloat16 or wider, within the bound.
A program may use at most 64 MiB of HBM per device.

v0:
```python
from functools import partial
import math

import jax
import jax.numpy as jnp
from jax import lax
from jax.sharding import PartitionSpec as P

ROPE = 64
NOPE = 128
VALUE_DIM = 128


EPSILON = 1e-06
NEGATIVE = -1e30


def rope_angle(positions, width):
    half_width = width // 2
    frequency = jnp.exp(-jnp.log(10000.0) * jnp.arange(half_width, dtype=jnp.float32) / half_width)
    return positions.astype(jnp.float32)[:, None] * frequency[None, :]


def rotate_pairs(values, angle):
    half_width = values.shape[-1] // 2
    first_half = values[..., :half_width]
    second = values[..., half_width:]
    cosine = jnp.cos(angle)
    sine_part = jnp.sin(angle)
    return jnp.concatenate(
        [first_half * cosine - second * sine_part, second * cosine + first_half * sine_part], -1
    )


def block_positions(begin_row, row_count, table, block_rows):
    row_ids = begin_row + jnp.arange(row_count, dtype=jnp.int32)
    blocks = row_ids // block_rows
    slot_ids = jnp.arange(table.shape[0], dtype=jnp.int32)
    looked = jnp.sum(jnp.where(blocks[:, None] == slot_ids[None, :], table[None, :], 0), axis=1)
    return looked * block_rows + row_ids % block_rows


def block_length(row_count, shard_rows):
    best_rows = shard_rows
    for factor in range(1, row_count // shard_rows + 1):
        if row_count // shard_rows % factor == 0 and shard_rows * factor <= max(512, shard_rows):
            best_rows = shard_rows * factor
    return best_rows


def attend_block(
    carried,
    query_latent,
    query_rotated,
    query_place,
    key_latent,
    key_rotated,
    key_place,
    score_scale,
):
    running_max, running_total, summed = carried
    contract = (((1,), (1,)), ((), ()))
    scores = lax.dot_general(query_latent, key_latent, contract, preferred_element_type=jnp.float32)
    scores = (
        scores
        + lax.dot_general(query_rotated, key_rotated, contract, preferred_element_type=jnp.float32)
    ) * score_scale
    visible = key_place[None, :] <= query_place[:, None]
    scores = jnp.where(visible, scores, NEGATIVE)
    new_max = jnp.maximum(running_max, jnp.max(scores, axis=1))
    exps = jnp.where(visible, jnp.exp(scores - new_max[:, None]), 0.0)
    shrink = jnp.exp(running_max - new_max)
    running_total = running_total * shrink + jnp.sum(exps, axis=1)
    summed = summed * shrink[:, None] + jnp.dot(
        exps.astype(jnp.bfloat16), key_latent, preferred_element_type=jnp.float32
    )
    return (new_max, running_total, summed)


def per_device(
    query_nope, query_rope, kv_latent, key_rope, latent_gain, w_key, w_value, block_order
):
    tokens_here = query_nope.shape[0]
    heads_here = w_key.shape[1] // NOPE
    latent_width = w_key.shape[0]
    block_rows = tokens_here // 2
    score_scale = 1.0 / math.sqrt(NOPE + ROPE)
    first_row = lax.axis_index("ctx") * tokens_here
    query_place = block_positions(first_row, tokens_here, block_order, block_rows)
    query_angle = rope_angle(query_place, ROPE)
    query_rotated = rotate_pairs(
        query_rope.astype(jnp.float32).reshape(tokens_here, heads_here, ROPE),
        query_angle[:, None, :],
    )
    query_rotated = query_rotated.astype(jnp.bfloat16).reshape(tokens_here * heads_here, ROPE)
    absorbed = jnp.einsum(
        "thd,lhd->thl",
        query_nope.reshape(tokens_here, heads_here, NOPE),
        w_key.reshape(latent_width, heads_here, NOPE),
        preferred_element_type=jnp.float32,
    )
    absorbed = absorbed.astype(jnp.bfloat16).reshape(tokens_here * heads_here, latent_width)
    row_place = jnp.repeat(query_place, heads_here)
    groups = ((absorbed, query_rotated, row_place),)
    initial = tuple(
        (
            (
                jnp.full((member[0].shape[0],), NEGATIVE, jnp.float32),
                jnp.zeros((member[0].shape[0],), jnp.float32),
                jnp.zeros((member[0].shape[0], latent_width), jnp.float32),
            )
            for member in groups
        )
    )
    columns = kv_latent.shape[1]
    column_part = kv_latent.astype(jnp.float32)
    square = lax.psum(jnp.sum(column_part * column_part, axis=1), "head")
    gain_part = lax.dynamic_slice_in_dim(latent_gain, lax.axis_index("head") * columns, columns, 0)
    scaled = (
        column_part * lax.rsqrt(square / latent_width + EPSILON)[:, None] * gain_part[None, :]
    ).astype(jnp.bfloat16)
    normed = lax.all_gather(scaled, "head", axis=1, tiled=True)
    key_rotated = rotate_pairs(key_rope.astype(jnp.float32), query_angle).astype(jnp.bfloat16)
    key_latent = lax.all_gather(normed, "ctx", axis=0, tiled=True)
    make_key_rotated = lax.all_gather(key_rotated, "ctx", axis=0, tiled=True)
    row_count = key_latent.shape[0]
    length = block_length(row_count, tokens_here)
    block_count = row_count // length
    latent_blocks = key_latent.reshape(block_count, length, latent_width)
    rotated_blocks = make_key_rotated.reshape(block_count, length, ROPE)
    block_starts = length * jnp.arange(block_count, dtype=jnp.int32)

    def one_block(state_now, operands):
        latent_block, rotated_block, first_key = operands
        key_place = block_positions(first_key, length, block_order, block_rows)
        updated = []
        for member, member_state in zip(groups, state_now):
            advance = partial(
                attend_block,
                query_latent=member[0],
                query_rotated=member[1],
                query_place=member[2],
                key_latent=latent_block,
                key_rotated=rotated_block,
                key_place=key_place,
                score_scale=score_scale,
            )
            updated.append(advance(member_state))
        return (tuple(updated), None)

    result, unused = lax.scan(one_block, initial, (latent_blocks, rotated_blocks, block_starts))
    mixed = jnp.concatenate(
        [
            (member_state[2] / member_state[1][:, None]).astype(jnp.bfloat16)
            for member_state in result
        ],
        0,
    )
    mixed = mixed.reshape(tokens_here, heads_here, latent_width)
    output = jnp.einsum(
        "thl,lhe->the",
        mixed,
        w_value.reshape(latent_width, heads_here, VALUE_DIM),
        preferred_element_type=jnp.float32,
    )
    return output.astype(jnp.bfloat16).reshape(tokens_here, heads_here * VALUE_DIM)


def solution(mesh):
    return jax.shard_map(
        per_device,
        mesh=mesh,
        in_specs=(
            P(("group", "ctx"), "head"),
            P(("group", "ctx"), "head"),
            P(("group", "ctx"), "head"),
            P(("group", "ctx"), None),
            P(),
            P(None, "head"),
            P(None, "head"),
            P("group"),
        ),
        out_specs=P(("group", "ctx"), "head"),
        check_vma=False,
    )
```

profile of v0, /device:TPU:33, one launch (start us, length us, event | category | flops | bytes accessed | tf_op | source)
XLA Modules:
  0.0 324.0 jit_solution(1167519836539736280)
XLA Ops:
  6.6 1.0 fusion.47
  7.5 9.7 %psum.7 = f32[64]{0:T(128)S(1)} all-reduce(f32[64]{0:T(128)S(1)} %fusion.47), channel_id=1, replica_groups=mesh['group'=2,'ctx'=64,'head'=4] {'head'}, use_global_device_ids=true, to_apply=%region_1.2 | all-reduce | flops 64 | bytes 512 | tf_op jit(solution)/shard_map/psum | solution.py:117
  17.3 0.8 dynamic_slice.24
  18.0 0.8 fusion.49
  18.8 8.6 %all_gather.9 = bf16[64,512]{1,0:T(8,128)(2,1)} all-gather(bf16[64,128]{1,0:T(8,128)(2,1)S(1)} %fusion.49), channel_id=1, replica_groups=mesh['group'=2,'ctx'=64,'head'=4] {'head'}, dimensions={1}, use_global_device_ids=true | all-gather | bytes 81920 | tf_op jit(solution)/shard_map/all_gather | solution.py:122
  27.5 0.7 convert_element_type.45
  28.2 1.9 reshape.179
  30.1 1.8 fusion.35
  33.0 1.4 subtract_convert_fusion
  34.7 109.5 %all_gather.11 = bf16[4096,64]{1,0:T(8,128)(2,1)} all-gather(bf16[64,64]{1,0:T(8,128)(2,1)S(1)} %pad_maximum_fusion.1), channel_id=1, replica_groups=mesh['group'=2,'ctx'=64,'head'=4] {'ctx'}, dimensions={0}, use_global_device_ids=true | all-gather | bytes 532480 | tf_op jit(solution)/shard_map/all_gather | solution.py:125
  144.2 49.3 %all-gather.2.cloned.1.call-done = bf16[4096,512]{1,0:T(8,128)(2,1)} async-done(((bf16[64,512]{1,0:T(8,128)(2,1)}), bf16[4096,512]{1,0:T(8,128)(2,1)}) %all-gather.2.cloned.1.call-update) | async-done | bytes 4194320 | tf_op jit(solution)/shard_map/all_gather | solution.py:124
  193.4 119.3 %while.17 = (s32[]{:T(128)}, f32[1024]{0:T(1024)S(1)}, f32[1024]{0:T(1024)S(1)}, f32[1024,512]{1,0:T(8,128)}, s32[8]{0:T(128)S(1)}, /*index=5*/s32[128]{0:T(128)...) while((s32[]{:T(128)}, f32[1024]{0:T(1024)S(1)}, ...), condition=%wide.region_7.8_spmd.clone, body=%wide.region_3.7_spmd.clone.sunk | while | flops 1149455872 | bytes 25536952 | solution.py:151
  195.4 2.7 fusion.75
  198.3 3.9 %fusion.77 = (f32[1024]{0:T(1024)S(1)}, f32[1024,512]{0,1:T(8,128)}) fusion(f32[512,1024]{1,0:T(8,128)} %fusion.75, bf16[1024,512]{1,0:T(8,128)(2,1)S(1)} %get-tuple-element.331, bf16[8,512,512]{2,1,0:T(8,128)(2,1)} %get-tuple-element.330, s32[]{:T(128)} %get-tuple-element.311, s32[1024]{0:T(1024)S(1)} %le.64, s32[512]{0:T(512)S(1)} %fusion.76), kind=kOutput, calls=%fused_computation.80.clone.1 | convolution fusion | flops 539491328 | bytes 5777920 | tf_op jit(solution)/shard_map/while/body/eval_jaxpr/dot_general | solution.py:63
  202.2 2.2 fusion.78
  204.4 3.3 %fusion.80 = f32[1024,512]{1,0:T(8,128)} fusion(f32[1024,512]{1,0:T(8,128)} %get-tuple-element.314, f32[1024,512]{0,1:T(8,128)S(1)} %copy-done.1, f32[1024]{0:T(1024)S(1)} %get-tuple-element.297, f32[1024]{0:T(1024)S(1)} %select_maximum_fusion.2, s32[1024]{0:T(1024)S(1)} %le.64, s32[512]{0:T(512)S(1)} %fusion.76, pred[]{:T(512)S(6)} %compare.27, ...), kind=kOutput, calls=%fused_computation.4.clone.1 | convolution fusion | flops 540540928 | bytes 6830593 | tf_op jit(solution)/shard_map/while/body/eval_jaxpr/dot_general | solution.py:74
  209.7 2.7 fusion.75
  212.6 3.9 %fusion.77 = (f32[1024]{0:T(1024)S(1)}, f32[1024,512]{0,1:T(8,128)}) fusion(f32[512,1024]{1,0:T(8,128)} %fusion.75, bf16[1024,512]{1,0:T(8,128)(2,1)S(1)} %get-tuple-element.331, bf16[8,512,512]{2,1,0:T(8,128)(2,1)} %get-tuple-element.330, s32[]{:T(128)} %get-tuple-element.311, s32[1024]{0:T(1024)S(1)} %le.64, s32[512]{0:T(512)S(1)} %fusion.76), kind=kOutput, calls=%fused_computation.80.clone.1 | convolution fusion | flops 539491328 | bytes 5777920 | tf_op jit(solution)/shard_map/while/body/eval_jaxpr/dot_general | solution.py:63
  216.5 2.2 fusion.78
  218.7 4.0 %fusion.80 = f32[1024,512]{1,0:T(8,128)} fusion(f32[1024,512]{1,0:T(8,128)} %get-tuple-element.314, f32[1024,512]{0,1:T(8,128)S(1)} %copy-done.1, f32[1024]{0:T(1024)S(1)} %get-tuple-element.297, f32[1024]{0:T(1024)S(1)} %select_maximum_fusion.2, s32[1024]{0:T(1024)S(1)} %le.64, s32[512]{0:T(512)S(1)} %fusion.76, pred[]{:T(512)S(6)} %compare.27, ...), kind=kOutput, calls=%fused_computation.4.clone.1 | convolution fusion | flops 540540928 | bytes 6830593 | tf_op jit(solution)/shard_map/while/body/eval_jaxpr/dot_general | solution.py:74
  224.7 2.7 fusion.75
  227.6 3.9 %fusion.77 = (f32[1024]{0:T(1024)S(1)}, f32[1024,512]{0,1:T(8,128)}) fusion(f32[512,1024]{1,0:T(8,128)} %fusion.75, bf16[1024,512]{1,0:T(8,128)(2,1)S(1)} %get-tuple-element.331, bf16[8,512,512]{2,1,0:T(8,128)(2,1)} %get-tuple-element.330, s32[]{:T(128)} %get-tuple-element.311, s32[1024]{0:T(1024)S(1)} %le.64, s32[512]{0:T(512)S(1)} %fusion.76), kind=kOutput, calls=%fused_computation.80.clone.1 | convolution fusion | flops 539491328 | bytes 5777920 | tf_op jit(solution)/shard_map/while/body/eval_jaxpr/dot_general | solution.py:63
  231.5 2.2 fusion.78
  233.7 4.0 %fusion.80 = f32[1024,512]{1,0:T(8,128)} fusion(f32[1024,512]{1,0:T(8,128)} %get-tuple-element.314, f32[1024,512]{0,1:T(8,128)S(1)} %copy-done.1, f32[1024]{0:T(1024)S(1)} %get-tuple-element.297, f32[1024]{0:T(1024)S(1)} %select_maximum_fusion.2, s32[1024]{0:T(1024)S(1)} %le.64, s32[512]{0:T(512)S(1)} %fusion.76, pred[]{:T(512)S(6)} %compare.27, ...), kind=kOutput, calls=%fused_computation.4.clone.1 | convolution fusion | flops 540540928 | bytes 6830593 | tf_op jit(solution)/shard_map/while/body/eval_jaxpr/dot_general | solution.py:74
  239.7 2.7 fusion.75
  242.6 3.9 %fusion.77 = (f32[1024]{0:T(1024)S(1)}, f32[1024,512]{0,1:T(8,128)}) fusion(f32[512,1024]{1,0:T(8,128)} %fusion.75, bf16[1024,512]{1,0:T(8,128)(2,1)S(1)} %get-tuple-element.331, bf16[8,512,512]{2,1,0:T(8,128)(2,1)} %get-tuple-element.330, s32[]{:T(128)} %get-tuple-element.311, s32[1024]{0:T(1024)S(1)} %le.64, s32[512]{0:T(512)S(1)} %fusion.76), kind=kOutput, calls=%fused_computation.80.clone.1 | convolution fusion | flops 539491328 | bytes 5777920 | tf_op jit(solution)/shard_map/while/body/eval_jaxpr/dot_general | solution.py:63
  246.5 2.2 fusion.78
  248.7 4.0 %fusion.80 = f32[1024,512]{1,0:T(8,128)} fusion(f32[1024,512]{1,0:T(8,128)} %get-tuple-element.314, f32[1024,512]{0,1:T(8,128)S(1)} %copy-done.1, f32[1024]{0:T(1024)S(1)} %get-tuple-element.297, f32[1024]{0:T(1024)S(1)} %select_maximum_fusion.2, s32[1024]{0:T(1024)S(1)} %le.64, s32[512]{0:T(512)S(1)} %fusion.76, pred[]{:T(512)S(6)} %compare.27, ...), kind=kOutput, calls=%fused_computation.4.clone.1 | convolution fusion | flops 540540928 | bytes 6830593 | tf_op jit(solution)/shard_map/while/body/eval_jaxpr/dot_general | solution.py:74
  254.7 2.7 fusion.75
  257.6 3.9 %fusion.77 = (f32[1024]{0:T(1024)S(1)}, f32[1024,512]{0,1:T(8,128)}) fusion(f32[512,1024]{1,0:T(8,128)} %fusion.75, bf16[1024,512]{1,0:T(8,128)(2,1)S(1)} %get-tuple-element.331, bf16[8,512,512]{2,1,0:T(8,128)(2,1)} %get-tuple-element.330, s32[]{:T(128)} %get-tuple-element.311, s32[1024]{0:T(1024)S(1)} %le.64, s32[512]{0:T(512)S(1)} %fusion.76), kind=kOutput, calls=%fused_computation.80.clone.1 | convolution fusion | flops 539491328 | bytes 5777920 | tf_op jit(solution)/shard_map/while/body/eval_jaxpr/dot_general | solution.py:63
  261.5 2.2 fusion.78
  263.7 4.0 %fusion.80 = f32[1024,512]{1,0:T(8,128)} fusion(f32[1024,512]{1,0:T(8,128)} %get-tuple-element.314, f32[1024,512]{0,1:T(8,128)S(1)} %copy-done.1, f32[1024]{0:T(1024)S(1)} %get-tuple-element.297, f32[1024]{0:T(1024)S(1)} %select_maximum_fusion.2, s32[1024]{0:T(1024)S(1)} %le.64, s32[512]{0:T(512)S(1)} %fusion.76, pred[]{:T(512)S(6)} %compare.27, ...), kind=kOutput, calls=%fused_computation.4.clone.1 | convolution fusion | flops 540540928 | bytes 6830593 | tf_op jit(solution)/shard_map/while/body/eval_jaxpr/dot_general | solution.py:74
  269.7 2.7 fusion.75
  272.6 3.9 %fusion.77 = (f32[1024]{0:T(1024)S(1)}, f32[1024,512]{0,1:T(8,128)}) fusion(f32[512,1024]{1,0:T(8,128)} %fusion.75, bf16[1024,512]{1,0:T(8,128)(2,1)S(1)} %get-tuple-element.331, bf16[8,512,512]{2,1,0:T(8,128)(2,1)} %get-tuple-element.330, s32[]{:T(128)} %get-tuple-element.311, s32[1024]{0:T(1024)S(1)} %le.64, s32[512]{0:T(512)S(1)} %fusion.76), kind=kOutput, calls=%fused_computation.80.clone.1 | convolution fusion | flops 539491328 | bytes 5777920 | tf_op jit(solution)/shard_map/while/body/eval_jaxpr/dot_general | solution.py:63
  276.5 2.2 fusion.78
  278.7 4.0 %fusion.80 = f32[1024,512]{1,0:T(8,128)} fusion(f32[1024,512]{1,0:T(8,128)} %get-tuple-element.314, f32[1024,512]{0,1:T(8,128)S(1)} %copy-done.1, f32[1024]{0:T(1024)S(1)} %get-tuple-element.297, f32[1024]{0:T(1024)S(1)} %select_maximum_fusion.2, s32[1024]{0:T(1024)S(1)} %le.64, s32[512]{0:T(512)S(1)} %fusion.76, pred[]{:T(512)S(6)} %compare.27, ...), kind=kOutput, calls=%fused_computation.4.clone.1 | convolution fusion | flops 540540928 | bytes 6830593 | tf_op jit(solution)/shard_map/while/body/eval_jaxpr/dot_general | solution.py:74
  284.7 2.7 fusion.75
  287.6 3.9 %fusion.77 = (f32[1024]{0:T(1024)S(1)}, f32[1024,512]{0,1:T(8,128)}) fusion(f32[512,1024]{1,0:T(8,128)} %fusion.75, bf16[1024,512]{1,0:T(8,128)(2,1)S(1)} %get-tuple-element.331, bf16[8,512,512]{2,1,0:T(8,128)(2,1)} %get-tuple-element.330, s32[]{:T(128)} %get-tuple-element.311, s32[1024]{0:T(1024)S(1)} %le.64, s32[512]{0:T(512)S(1)} %fusion.76), kind=kOutput, calls=%fused_computation.80.clone.1 | convolution fusion | flops 539491328 | bytes 5777920 | tf_op jit(solution)/shard_map/while/body/eval_jaxpr/dot_general | solution.py:63
  291.5 2.2 fusion.78
  293.7 4.0 %fusion.80 = f32[1024,512]{1,0:T(8,128)} fusion(f32[1024,512]{1,0:T(8,128)} %get-tuple-element.314, f32[1024,512]{0,1:T(8,128)S(1)} %copy-done.1, f32[1024]{0:T(1024)S(1)} %get-tuple-element.297, f32[1024]{0:T(1024)S(1)} %select_maximum_fusion.2, s32[1024]{0:T(1024)S(1)} %le.64, s32[512]{0:T(512)S(1)} %fusion.76, pred[]{:T(512)S(6)} %compare.27, ...), kind=kOutput, calls=%fused_computation.4.clone.1 | convolution fusion | flops 540540928 | bytes 6830593 | tf_op jit(solution)/shard_map/while/body/eval_jaxpr/dot_general | solution.py:74
  297.7 0.6 dynamic_slice.49
  299.7 2.7 fusion.75
  302.6 3.9 %fusion.77 = (f32[1024]{0:T(1024)S(1)}, f32[1024,512]{0,1:T(8,128)}) fusion(f32[512,1024]{1,0:T(8,128)} %fusion.75, bf16[1024,512]{1,0:T(8,128)(2,1)S(1)} %get-tuple-element.331, bf16[8,512,512]{2,1,0:T(8,128)(2,1)} %get-tuple-element.330, s32[]{:T(128)} %get-tuple-element.311, s32[1024]{0:T(1024)S(1)} %le.64, s32[512]{0:T(512)S(1)} %fusion.76), kind=kOutput, calls=%fused_computation.80.clone.1 | convolution fusion | flops 539491328 | bytes 5777920 | tf_op jit(solution)/shard_map/while/body/eval_jaxpr/dot_general | solution.py:63
  306.5 2.2 fusion.78
  308.7 4.0 %fusion.80 = f32[1024,512]{1,0:T(8,128)} fusion(f32[1024,512]{1,0:T(8,128)} %get-tuple-element.314, f32[1024,512]{0,1:T(8,128)S(1)} %copy-done.1, f32[1024]{0:T(1024)S(1)} %get-tuple-element.297, f32[1024]{0:T(1024)S(1)} %select_maximum_fusion.2, s32[1024]{0:T(1024)S(1)} %le.64, s32[512]{0:T(512)S(1)} %fusion.76, pred[]{:T(512)S(6)} %compare.27, ...), kind=kOutput, calls=%fused_computation.4.clone.1 | convolution fusion | flops 540540928 | bytes 6830593 | tf_op jit(solution)/shard_map/while/body/eval_jaxpr/dot_general | solution.py:74
  312.7 1.9 divide_convert_fusion
  314.9 1.5 fusion.41
  316.4 0.8 copy.52
  (108 shorter events, 18.4 us)
Async XLA Ops:
  6.5 23.6 %copy-start = (bf16[512,2048]{1,0:T(8,128)(2,1)S(1)}, bf16[512,2048]{1,0:T(8,128)(2,1)}, u32[]{:S(2)}) copy-start(bf16[512,2048]{1,0:T(8,128)(2,1)} %param.15) | copy-start | bytes 6291460
  6.6 186.9 %all-gather.2.cloned.1.call-start = ((), (), s32[]{:S(2)}) async-start(), calls=%async_computation | async-start | bytes 4259840 | tf_op jit(solution)/shard_map/all_gather | solution.py:124
  30.1 2.4 copy-start.2
  202.2 2.2 copy-start.1
  216.5 2.2 copy-start.1
  231.5 2.2 copy-start.1
  246.5 2.2 copy-start.1
  261.5 2.2 copy-start.1
  276.5 2.2 copy-start.1
  291.5 2.2 copy-start.1
  306.5 2.2 copy-start.1
  312.7 2.2 copy-start.3
Sparse Core Ops, SparseCore 0:
  27.6 165.7 all-gather.1
where the time goes:
time: 325 us; the launch traced here: 324 us
  blocking collectives  128 us (39%)
  matrix products  87.6 us (27%)
  waiting for transfers between devices  49.3 us (15%)
  other arithmetic  35.2 us (11%)
  between operations  13.5 us (4%)
  local copies, waits for them, and re-layouts  10.3 us (3%)
    all_gather x1, blocking collectives, per_device(): make_key_rotated = lax.all_gather(key_rotated, 'ctx', axis=0, tiled=True)  110 us
    all_gather x1, waiting for transfers between devices, per_device(): key_latent = lax.all_gather(normed, 'ctx', axis=0, tiled=True)  49.3 us
    dot_general x8, matrix products, attend_block(): lax.dot_general(query_latent, key_latent, contract, preferred_element_typ...  31.4 us
    dot_general x8, matrix products, attend_block(): jnp.dot(exps.astype(jnp.bfloat16), key_latent, preferred_element_type=jnp...  31.3 us
    dot_general x8, matrix products, attend_block(): lax.dot_general(query_rotated, key_rotated, contract, preferred_element_t...  21.5 us
    reduce_sum x8, other arithmetic, attend_block(): running_total = running_total * shrink + jnp.sum(exps, axis=1)  17.4 us
    psum x1, blocking collectives, per_device(): square = lax.psum(jnp.sum(column_part * column_part, axis=1), 'head')  9.74 us
    all_gather x1, blocking collectives, per_device(): normed = lax.all_gather(scaled, 'head', axis=1, tiled=True)  8.6 us
  transfers between devices with their start and end apart: 1, of which 1 were waited for; matrix products, arithmetic and copies ran while one was open for 2% of the time, Pallas kernels for 0%

commit v1 on v0

v1 whole, which is shorter than its diff:
```python
import functools
import math

import jax
import jax.numpy as jnp
from jax import lax
from jax.experimental import pallas as pl
from jax.experimental.pallas import tpu as pltpu
from jax.sharding import PartitionSpec as P

ROPE = 64
NOPE = 128
VALUE_DIM = 128
EPSILON = 1e-06
NEGATIVE = -1e30
LANES = 128
TILE = 256
NT = (((1,), (1,)), ((), ()))
SCORE_SCALE = math.log2(math.e) / math.sqrt(NOPE + ROPE)


def rotate_rows(values, position):
    lane = lax.broadcasted_iota(jnp.int32, values.shape, 1)
    half = ROPE // 2
    index = lax.rem(lane, half).astype(jnp.float32)
    angle = position.astype(jnp.float32) * jnp.exp(-math.log(10000.0) * index / half)
    low = lax.rem(lane, ROPE) < half
    partner = jnp.where(
        low, pltpu.roll(values, LANES - half, 1), pltpu.roll(values, half, 1)
    )
    sine = jnp.sin(angle)
    return values * jnp.cos(angle) + partner * jnp.where(low, -sine, sine)


def attend_kernel(
    heads,
    order_ref,
    q_nope_ref,
    q_rope_ref,
    w_key_hbm,
    w_value_hbm,
    keys_hbm,
    out_ref,
    w_key,
    w_value,
    keys,
    queries,
    scores,
    total_max,
    total_sum,
    mixed,
    key_sem,
    weight_sem,
):
    tokens, block = q_nope_ref.shape[0], q_nope_ref.shape[0] // 2
    latent = w_key.shape[0]
    rows = heads * block
    blocks = order_ref.shape[0]
    load_w_key = pltpu.make_async_copy(w_key_hbm, w_key, weight_sem.at[0])
    load_w_value = pltpu.make_async_copy(w_value_hbm, w_value, weight_sem.at[1])
    load_w_key.start()

    def load_block(row_block, carry):
        place = order_ref[row_block]
        pltpu.make_async_copy(
            keys_hbm.at[pl.ds(pl.multiple_of(row_block * block, block), block)],
            keys.at[pl.ds(pl.multiple_of(place * block, block), block)],
            key_sem,
        ).start()
        return carry

    lax.fori_loop(0, blocks, load_block, 0)
    load_w_value.start()

    here = lax.axis_index("ctx")
    places = (order_ref[2 * here], order_ref[2 * here + 1])
    row = lax.broadcasted_iota(jnp.int32, (tokens, LANES), 0)
    position = jnp.where(
        row < block, places[0] * block + row, places[1] * block + row - block
    )
    lane = lax.broadcasted_iota(jnp.int32, (tokens, LANES), 1)
    for pair in range(heads // 2):
        turned = rotate_rows(
            q_rope_ref[:, pair * LANES : (pair + 1) * LANES].astype(jnp.float32), position
        )
        turned = turned * SCORE_SCALE
        for side in range(2):
            head = 2 * pair + side
            alone = turned if side == 0 else pltpu.roll(turned, ROPE, 1)
            alone = jnp.where(lane < ROPE, alone, 0.0).astype(jnp.bfloat16)
            for member in range(2):
                queries[pl.ds(member * rows + head * block, block), latent:] = alone[
                    member * block : (member + 1) * block
                ]
    load_w_key.wait()
    for head in range(heads):
        columns = slice(head * NOPE, (head + 1) * NOPE)
        absorbed = lax.dot_general(
            q_nope_ref[:, columns], w_key[:, columns], NT, preferred_element_type=jnp.float32
        )
        absorbed = (absorbed * SCORE_SCALE).astype(jnp.bfloat16)
        for member in range(2):
            queries[pl.ds(member * rows + head * block, block), :latent] = absorbed[
                member * block : (member + 1) * block
            ]
    total_max[...] = jnp.full_like(total_max, NEGATIVE)
    total_sum[...] = jnp.zeros_like(total_sum)
    mixed[...] = jnp.zeros_like(mixed)
    pltpu.make_async_copy(keys_hbm, keys, key_sem).wait()

    per_tile = TILE // block
    first_tiles = places[0] // per_tile + 1
    tiles = first_tiles + places[1] // per_tile + 1

    def tile_of(step):
        second = step >= first_tiles
        member = second.astype(jnp.int32)
        tile = jnp.where(second, step - first_tiles, step)
        return member, tile

    def score(step):
        member, tile = tile_of(step)
        return lax.dot_general(
            queries[pl.ds(pl.multiple_of(member * rows, rows), rows), :],
            keys[pl.ds(pl.multiple_of(tile * TILE, TILE), TILE), :],
            NT,
            preferred_element_type=jnp.float32,
        )

    shift = lax.broadcasted_iota(jnp.int32, (block, TILE), 1) - lax.broadcasted_iota(
        jnp.int32, (block, TILE), 0
    )
    scores[0] = score(0)

    def one_step(step, carry):
        now = lax.rem(step, 2)
        member, tile = tile_of(step)
        here_rows = pl.ds(pl.multiple_of(member * rows, rows), rows)
        ahead = jnp.minimum(step + 1, tiles - 1)
        scores[1 - now] = score(ahead)
        place = jnp.where(member == 1, places[1], places[0])
        bound = place * block - tile * TILE
        visible = jnp.broadcast_to((shift <= bound)[None], (heads, block, TILE)).reshape(rows, TILE)
        part = jnp.where(visible, scores[now], NEGATIVE)
        before = total_max[here_rows]
        after = jnp.maximum(before, jnp.max(part, axis=1, keepdims=True))
        exps = jnp.exp2(part - jnp.concatenate([after] * (TILE // LANES), 1))
        shrink = jnp.exp2(before - after)
        total_max[here_rows] = after
        sums = exps[:, :LANES]
        for piece in range(1, TILE // LANES):
            sums = sums + exps[:, piece * LANES : (piece + 1) * LANES]
        total_sum[here_rows] = total_sum[here_rows] * shrink + sums
        gained = jnp.dot(
            exps.astype(jnp.bfloat16),
            keys[pl.ds(pl.multiple_of(tile * TILE, TILE), TILE), :latent],
            preferred_element_type=jnp.float32,
        )
        mixed[here_rows] = (
            mixed[here_rows] * jnp.concatenate([shrink] * (latent // LANES), 1) + gained
        )
        return carry

    lax.fori_loop(0, tiles, one_step, 0)
    load_w_value.wait()
    for head in range(heads):
        parts = []
        for member in range(2):
            at = pl.ds(member * rows + head * block, block)
            inverse = 1.0 / jnp.sum(total_sum[at], axis=1, keepdims=True)
            parts.append((mixed[at] * inverse).astype(jnp.bfloat16))
        columns = slice(head * VALUE_DIM, (head + 1) * VALUE_DIM)
        out_ref[:, columns] = jnp.dot(
            jnp.concatenate(parts, 0), w_value[:, columns], preferred_element_type=jnp.float32
        ).astype(jnp.bfloat16)


def attend(block_order, query_nope, query_rope, w_key, w_value, keys):
    tokens = query_nope.shape[0]
    heads = w_key.shape[1] // NOPE
    latent = w_key.shape[0]
    width = keys.shape[1]
    vmem = pl.BlockSpec(memory_space=pltpu.VMEM)
    hbm = pl.BlockSpec(memory_space=pl.ANY)
    return pl.pallas_call(
        functools.partial(attend_kernel, heads),
        out_shape=jax.ShapeDtypeStruct((tokens, w_value.shape[1]), jnp.bfloat16),
        in_specs=[pl.BlockSpec(memory_space=pltpu.SMEM), vmem, vmem, hbm, hbm, hbm],
        out_specs=vmem,
        scratch_shapes=[
            pltpu.VMEM(w_key.shape, jnp.bfloat16),
            pltpu.VMEM(w_value.shape, jnp.bfloat16),
            pltpu.VMEM(keys.shape, jnp.bfloat16),
            pltpu.VMEM((tokens * heads, width), jnp.bfloat16),
            pltpu.VMEM((2, tokens * heads // 2, TILE), jnp.float32),
            pltpu.VMEM((tokens * heads, LANES), jnp.float32),
            pltpu.VMEM((tokens * heads, LANES), jnp.float32),
            pltpu.VMEM((tokens * heads, latent), jnp.float32),
            pltpu.SemaphoreType.DMA,
            pltpu.SemaphoreType.DMA((2,)),
        ],
        compiler_params=pltpu.CompilerParams(vmem_limit_bytes=56 * 1024 * 1024),
        name="attend",
    )(block_order, query_nope, query_rope, w_key, w_value, keys)


def per_device(
    query_nope, query_rope, kv_latent, key_rope, latent_gain, w_key, w_value, block_order
):
    tokens = query_nope.shape[0]
    latent = w_key.shape[0]
    block = tokens // 2
    columns = kv_latent.shape[1]
    order = lax.dynamic_slice_in_dim(block_order, 2 * lax.axis_index("ctx"), 2, 0)
    place = (order[:, None] * block + jnp.arange(block, dtype=jnp.int32)[None]).reshape(tokens)
    half = ROPE // 2
    frequency = jnp.exp(-jnp.log(10000.0) * jnp.arange(half, dtype=jnp.float32) / half)
    angle = place.astype(jnp.float32)[:, None] * frequency[None]
    low, high = jnp.split(key_rope.astype(jnp.float32), 2, 1)
    cosine, sine = jnp.cos(angle), jnp.sin(angle)
    turned = jnp.concatenate([low * cosine - high * sine, high * cosine + low * sine], 1)
    column_part = kv_latent.astype(jnp.float32)
    square = lax.psum(jnp.sum(column_part * column_part, axis=1), "head")
    gain_part = lax.dynamic_slice_in_dim(latent_gain, lax.axis_index("head") * columns, columns, 0)
    scaled = (
        column_part * lax.rsqrt(square / latent + EPSILON)[:, None] * gain_part[None, :]
    ).astype(jnp.bfloat16)
    normed = lax.all_gather(scaled, "head", axis=1, tiled=True)
    mine = jnp.concatenate(
        [normed, turned.astype(jnp.bfloat16), jnp.zeros((tokens, LANES - ROPE), jnp.bfloat16)], 1
    )
    keys = lax.all_gather(mine, "ctx", axis=0, tiled=True)
    return attend(block_order, query_nope, query_rope, w_key, w_value, keys)


def solution(mesh):
    return jax.shard_map(
        per_device,
        mesh=mesh,
        in_specs=(
            P(("group", "ctx"), "head"),
            P(("group", "ctx"), "head"),
            P(("group", "ctx"), "head"),
            P(("group", "ctx"), None),
            P(),
            P(None, "head"),
            P(None, "head"),
            P("group"),
        ),
        out_specs=P(("group", "ctx"), "head"),
        check_vma=False,
    )
```

time: 325 us -> 227 us (0.70)
  waiting for transfers between devices: 49.3 us -> 167 us
  blocking collectives: 128 us -> 17.9 us
  matrix products: 87.6 us -> 0 us
  other arithmetic: 35.2 us -> 4.07 us
  Pallas kernels: 0 us -> 23.4 us
  local copies, waits for them, and re-layouts: 10.3 us -> 0.92 us
    all_gather x1, waiting for transfers between devices: 49.3 us -> 166 us  [per_device(): keys = lax.all_gather(mine, 'ctx', axis=0, tiled=True)]
    all_gather x1 -> x0, blocking collectives: 110 us -> none  [per_device(): make_key_rotated = lax.all_gather(key_rotated, 'ctx', axis=0, tiled=True)]
    dot_general x26 -> x0, matrix products: 87.6 us -> none  [the longest x8 31.4 us: attend_block(): lax.dot_general(query_latent, key_latent, contract, preferred_element_typ...]
    pallas_call x0 -> x1, Pallas kernels: none -> 23.4 us  [attend(): pl.pallas_call(functools.partial(attend_kernel, heads), out_shape=jax.Sha...]
    reduce_sum x17 -> x0, other arithmetic: 19.4 us -> none  [the longest x8 17.4 us: attend_block(): running_total = running_total * shrink + jnp.sum(exps, axis=1)]
    add x16 -> x0, other arithmetic: 4.79 us -> none  [the longest x8 4.69 us: block_positions(): return looked * block_rows + row_ids % block_rows]
    dynamic_slice x8 -> x0, local copies, waits for them, and re-layouts: 4.69 us -> none  [per_device(): lax.scan(one_block, initial, (latent_blocks, rotated_blocks, block_starts))]
    select_n x9 -> x0, other arithmetic: 4.66 us -> none  [block_positions(): blocks = row_ids // block_rows]
  transfers between devices with their start and end apart: 1 -> 1, of which waited for: 1 -> 1; matrix products, arithmetic and copies ran while one was open for 2% -> 0% of each run, Pallas kernels for 0% -> 0%
where the time goes in v1:
time: 227 us; the launch traced here: 226 us
  waiting for transfers between devices  167 us (74%)
  Pallas kernels  23.4 us (10%)
  blocking collectives  17.9 us (8%)
  between operations  13.5 us (6%)
  other arithmetic  4.07 us (2%)
    all_gather x1, waiting for transfers between devices, per_device(): keys = lax.all_gather(mine, 'ctx', axis=0, tiled=True)  166 us
    pallas_call x1, Pallas kernels, attend(): pl.pallas_call(functools.partial(attend_kernel, heads), out_shape=jax.Sha...  23.4 us
    psum x1, blocking collectives, per_device(): square = lax.psum(jnp.sum(column_part * column_part, axis=1), 'head')  9.74 us
    all_gather x1, blocking collectives, per_device(): normed = lax.all_gather(scaled, 'head', axis=1, tiled=True)  8.18 us
  transfers between devices with their start and end apart: 1, of which 1 were waited for; matrix products, arithmetic and copies ran while one was open for 0% of the time, Pallas kernels for 0%

profile of v1, /device:TPU:33, one launch (start us, length us, event | category | flops | bytes accessed | tf_op | source)
XLA Modules:
  0.0 226.3 jit_solution(7062398105650692692)
XLA Ops:
  6.5 0.0 all-gather.2.cloned.1.call-start
  6.6 0.7 dynamic-slice_multiply_fusion
  7.3 0.1 add_convert_fusion
  7.4 0.1 convert_element_type.24
  7.5 0.8 fusion.4
  8.3 9.7 %psum.7 = f32[64]{0:T(128)S(1)} all-reduce(f32[64]{0:T(128)S(1)} %fusion.4), channel_id=1, replica_groups=mesh['group'=2,'ctx'=64,'head'=4] {'head'}, use_global_device_ids=true, to_apply=%region_1.0 | all-reduce | flops 64 | bytes 512 | tf_op jit(solution)/shard_map/psum | solution.py:223
  18.0 0.7 convert_element_type.22
  18.7 0.8 dynamic_slice.6
  19.5 0.8 fusion.6
  20.3 8.2 %all_gather.6 = bf16[64,512]{1,0:T(8,128)(2,1)S(1)} all-gather(bf16[64,128]{1,0:T(8,128)(2,1)S(1)} %fusion.6), channel_id=1, replica_groups=mesh['group'=2,'ctx'=64,'head'=4] {'head'}, dimensions={1}, use_global_device_ids=true | all-gather | bytes 81920 | tf_op jit(solution)/shard_map/all_gather | solution.py:228
  28.5 0.1 pad.3.clone
  28.6 0.2 fusion.8
  28.8 0.7 maximum_maximum_fusion
  29.5 0.1 all-gather.2.cloned.1.call-update
  29.5 166.5 %all-gather.2.cloned.1.call-done.keys_hbm = bf16[4096,640]{1,0:T(8,128)(2,1)} async-done(((bf16[64,640]{1,0:T(8,128)(2,1)}), bf16[4096,640]{1,0:T(8,128)(2,1)}) %all-gather.2.cloned.1.call-update) | async-done | bytes 5242896 | tf_op jit(solution)/shard_map/all_gather | solution.py:232
  196.0 23.4 %attend.1 = bf16[64,2048]{1,0:T(8,128)(2,1)} custom-call(s32[128]{0:T(128)} %order_ref.1, bf16[64,2048]{1,0:T(8,128)(2,1)} %q_nope_ref.1, bf16[64,1024]{1,0:T(8,128)(2,1)} %q_rope_ref.1, bf16[512,2048]{1,0:T(8,128)(2,1)} %w_key_hbm.1, bf16[512,2048]{1,0:T(8,128)(2,1)} %w_value_hbm.1, bf16[4096,640]{1,0:T(8,128)(2,1)} %all-gather.2.cloned.1.call-done.keys_hbm), custom_call_target="tpu_custom_call" | custom-call | tf_op jit(solution)/shard_map/attend/pallas_call | solution.py:185
  (3 shorter events, 0.0 us)
Async XLA Ops:
  6.5 189.5 %all-gather.2.cloned.1.call-start = ((), (), s32[]{:S(2)}) async-start(), calls=%async_computation | async-start | bytes 5324800 | tf_op jit(solution)/shard_map/all_gather | solution.py:232
Sparse Core Ops, SparseCore 0:
  29.7 166.2 all-gather.1
